TPU v7x, 32 devices: a whole 2x2x4 slice. The times are simulated.
32 devices in a mesh: rep: 2 (over y), tp: 4 (over z), ep: 4 (over x, core).
Axes of the slice: x: 2, y: 2, z: 4, core: 2. Of those that a mesh axis runs over, the one named last changes fastest.
Arguments:
- tokens: bfloat16 [768, 3072], P(('rep', 'ep'), 'tp'), parts along dimension 0, may hold values from -6 to 6
- routing: int32 [768, 2], P(('rep', 'ep')), parts along dimension 0, may hold values from 0 to 3, all different within a row; in each aligned block of 96 rows (0 to 95, 96 to 191, ...) at most 54 rows name the same one
- route_gates: float32 [768, 2], P(('rep', 'ep')), parts along dimension 0, may hold values from 0.2 to 1
- expert_gate: bfloat16 [4, 3072, 8192], P('ep', None, 'tp'), may hold values from -0.109375 to 0.109375
- expert_up: bfloat16 [4, 3072, 8192], P('ep', None, 'tp'), may hold values from -0.109375 to 0.109375
- expert_down: bfloat16 [4, 8192, 3072], P('ep', 'tp'), may hold values from -0.0625 to 0.0625
Outputs:
- mixture: bfloat16 [768, 3072], P(('rep', 'ep'), 'tp'), parts along dimension 0
There are 2 independent parts, one for each index of `rep`. A program takes and returns all parts, laid end to end along the dimension named above; an argument that names none is the same for every part. Nothing has to cross between parts.
Inputs may be any that keep to these rules, and one draw needn't show every extreme that they name: `routing`: each token names two different experts. In each aligned block of 96 tokens (the rows of one index of ep) no expert is named by more than 54 tokens, a bound that some block reaches.
All inputs are finite; a program needn't handle non-finite values.
Results may differ from a plain program's by a relative error of at most 0.0085.
Values may be sent and summed in bfloat16 or wider, within the bound.
A program may use at most 128 MiB of HBM per device.

v0:
```python
import jax
import jax.numpy as jnp
from jax import lax
from jax.sharding import PartitionSpec as P


def slot_tables(routing, route_gates, experts, capacity):
    count_rows = routing.shape[0]
    choices_n = routing.shape[1]
    flat_ids = routing.reshape(-1)
    onehot = (flat_ids[:, None] == jnp.arange(experts, dtype=jnp.int32)[None, :]).astype(jnp.int32)
    before = jnp.cumsum(onehot, axis=0) - onehot
    position = jnp.sum(before * onehot, axis=1)
    slot_index = flat_ids * capacity + position
    picked = (
        slot_index[:, None] == jnp.arange(experts * capacity, dtype=jnp.int32)[None, :]
    ).astype(jnp.float32)
    dispatch = picked.reshape(count_rows, choices_n, experts * capacity).sum(axis=1)
    combine = (
        (picked * route_gates.reshape(-1)[:, None])
        .reshape(count_rows, choices_n, experts * capacity)
        .sum(axis=1)
    )
    return (dispatch, combine)


def hidden_rows(everyone, expert_gate, expert_up, capacity):
    local_count = expert_gate.shape[0]
    total = everyone.shape[0]
    row_block = everyone.reshape(
        total // (local_count * capacity), local_count, capacity, everyone.shape[1]
    )
    gate_part = jnp.einsum(
        "tlcd,ldf->tlcf", row_block, expert_gate, preferred_element_type=jnp.float32
    )
    upward = jnp.einsum("tlcd,ldf->tlcf", row_block, expert_up, preferred_element_type=jnp.float32)
    return (jax.nn.silu(gate_part) * upward).astype(jnp.bfloat16)


def body(tokens, routing, route_gates, expert_gate, expert_up, expert_down):
    local_count = expert_gate.shape[0]
    ep_count = lax.axis_size("ep")
    tp_count = lax.axis_size("tp")
    tok_count = tokens.shape[0]
    capacity = 2 * tok_count // ep_count + tok_count // 16
    experts = local_count * ep_count
    dispatch, combine = slot_tables(routing, route_gates, experts, capacity)
    dispatch_low = dispatch.astype(jnp.bfloat16)
    whole = lax.all_gather(tokens, "tp", axis=1, tiled=True)
    packed = jnp.einsum(
        "tc,td->cd", dispatch_low, whole, preferred_element_type=jnp.float32
    ).astype(jnp.bfloat16)
    everyone = lax.all_to_all(packed, "ep", split_axis=0, concat_axis=0, tiled=True)
    total_rows = everyone.shape[0]
    columns = everyone.shape[1]
    hidden = hidden_rows(everyone, expert_gate, expert_up, capacity)
    part = jnp.einsum("tlcf,lfd->dtlc", hidden, expert_down, preferred_element_type=jnp.float32)
    summed_t = lax.psum_scatter(
        part.reshape(columns // tp_count * lax.axis_size("tp"), total_rows),
        "tp",
        scatter_dimension=0,
        tiled=True,
    )
    summed = summed_t.T
    expert_out = summed.astype(jnp.bfloat16)
    returned = lax.all_to_all(expert_out, "ep", split_axis=0, concat_axis=0, tiled=True)
    mixed = jnp.dot(combine, returned.astype(jnp.float32), precision=lax.Precision.HIGHEST)
    return mixed.astype(jnp.bfloat16)


def solution(mesh):
    return jax.shard_map(
        body,
        mesh=mesh,
        in_specs=(
            P(("rep", "ep"), "tp"),
            P(("rep", "ep"), None),
            P(("rep", "ep"), None),
            P("ep", None, "tp"),
            P("ep", None, "tp"),
            P("ep", "tp", None),
        ),
        out_specs=P(("rep", "ep"), "tp"),
        check_vma=False,
    )
```

profile of v0, /device:TPU:0, one launch (start us, length us, event | category | flops | bytes accessed | tf_op | source)
XLA Modules:
  0.0 145.9 jit_solution(12279673939200975978)
XLA Ops:
  6.5 0.0 reduce-scatter.2.cloned.1.call-start
  6.5 0.8 copy.23
  7.3 0.1 eq.37
  7.5 1.2 reduce-window.6
  8.7 0.1 slice.12
  8.8 0.1 copy.24
  8.9 0.1 copy.25
  9.0 0.1 add_bitcast_fusion
  9.1 0.1 reduce_sum.30
  9.3 0.1 copy.26
  9.3 0.7 multiply_add_fusion
  10.1 18.5 %all_gather.3 = bf16[96,3072]{1,0:T(8,128)(2,1)S(1)} all-gather(bf16[96,768]{1,0:T(8,128)(2,1)} %param.6), channel_id=1, replica_groups=mesh['rep'=2,'tp'=4,'ep'=4] {'tp'}, dimensions={1}, use_global_device_ids=true | all-gather | bytes 737280 | tf_op jit(solution)/shard_map/all_gather | solution.py:49
  28.5 0.8 convert_reduce_fusion
  29.3 0.5 convolution_convert_fusion
  29.9 0.4 all_to_all.14
  30.2 20.5 %all_to_all.21 = bf16[4,54,3072]{2,1,0:T(8,128)(2,1)S(1)} all-to-all(bf16[4,54,3072]{2,1,0:T(8,128)(2,1)S(1)} %all_to_all.14), channel_id=1, replica_groups=mesh['rep'=2,'tp'=4,'ep'=4] {'ep'}, dimensions={0} | all-to-all | bytes 2654208 | tf_op jit(solution)/shard_map/all_to_all | solution.py:53
  50.7 6.3 %fusion.9 = f32[4,1,54,2048]{3,2,0,1:T(8,128)S(1)} fusion(bf16[4,54,3072]{2,1,0:T(8,128)(2,1)S(1)} %all_to_all.21, bf16[1,3072,2048]{2,1,0:T(8,128)(2,1)} %param.9), kind=kOutput, calls=%fused_computation.8 | convolution fusion | flops 2717908992 | bytes 15679488 | tf_op jit(solution)/shard_map/tlcd,ldf->tlcf/dot_general | solution.py:33
  57.0 7.9 %fusion.18 = bf16[4,1,54,2048]{3,2,0,1:T(8,128)(2,1)S(1)} fusion(bf16[4,54,3072]{2,1,0:T(8,128)(2,1)S(1)} %all_to_all.21, bf16[1,3072,2048]{2,1,0:T(8,128)(2,1)} %param.10, f32[4,1,54,2048]{3,2,0,1:T(8,128)S(1)} %fusion.9), kind=kOutput, calls=%fused_computation.11 | convolution fusion | flops 2720563200 | bytes 16564224 | tf_op jit(solution)/shard_map/tlcd,ldf->tlcf/dot_general | solution.py:36
  64.9 0.2 dot_general.34
  65.1 9.0 %fusion.6 = f32[3072,216]{0,1:T(8,128)} fusion(bf16[216,2048]{1,0:T(8,128)(2,1)S(1)} %dot_general.34, bf16[1,2048,3072]{2,1,0:T(8,128)(2,1)} %param.11), kind=kOutput, calls=%fused_computation.6 | convolution fusion | flops 2717908992 | bytes 16121856 | tf_op jit(solution)/shard_map/tlcf,lfd->dtlc/dot_general | solution.py:57
  74.1 0.0 reduce-scatter.2.cloned.1.call-update
  74.2 53.2 %reduce-scatter.2.cloned.1.call-done = f32[768,216]{0,1:T(8,128)} async-done(((f32[3072,216]{0,1:T(8,128)}), f32[768,216]{0,1:T(8,128)}) %reduce-scatter.2.cloned.1.call-update) | async-done | bytes 663568 | tf_op jit(solution)/shard_map/reduce_scatter | solution.py:58
  127.4 1.1 convert_bitcast_fusion
  128.5 0.1 all_to_all.16
  128.6 9.4 %all_to_all.22 = bf16[4,54,768]{2,1,0:T(8,128)(2,1)S(1)} all-to-all(bf16[4,54,768]{2,1,0:T(8,128)(2,1)S(1)} %all_to_all.16), channel_id=1, replica_groups=mesh['rep'=2,'tp'=4,'ep'=4] {'ep'}, dimensions={0} | all-to-all | bytes 663552 | tf_op jit(solution)/shard_map/all_to_all | solution.py:66
  138.0 0.1 all_to_all.18
  138.1 1.0 convolution_convert_fusion.1
  (7 shorter events, 0.1 us)
Async XLA Ops:
  6.5 120.8 %reduce-scatter.2.cloned.1.call-start = ((), (), s32[]{:S(2)}) async-start(), calls=%async_computation.3 | async-start | bytes 3317760 | tf_op jit(solution)/shard_map/reduce_scatter | solution.py:58
Sparse Core Ops, SparseCore 0:
  74.3 53.0 reduce-scatter.1
where the time goes:
time: 146 us
  waiting for transfers between devices  53.2 us (36%)
  blocking collectives  48.4 us (33%)
  matrix products  24.6 us (17%)
  between operations  13.5 us (9%)
  other arithmetic  4.01 us (3%)
  local copies, waits for them, and re-layouts  2.2 us (2%)
    reduce_scatter x1, waiting for transfers between devices, body(): lax.psum_scatter(part.reshape(columns // tp_count * lax.axis_size('tp'),...  53.2 us
    all_to_all x1, blocking collectives, body(): lax.all_to_all(packed, 'ep', split_axis=0, concat_axis=0, tiled=True)  20.5 us
    all_gather x1, blocking collectives, body(): whole = lax.all_gather(tokens, 'tp', axis=1, tiled=True)  18.5 us
    all_to_all x1, blocking collectives, body(): lax.all_to_all(expert_out, 'ep', split_axis=0, concat_axis=0, tiled=True)  9.41 us
    dot_general x1, matrix products, body(): jnp.einsum('tlcf,lfd->dtlc', hidden, expert_down, preferred_element_type=...  9.01 us
    dot_general x1, matrix products, hidden_rows(): jnp.einsum('tlcd,ldf->tlcf', row_block, expert_up, preferred_element_type...  7.89 us
    dot_general x1, matrix products, hidden_rows(): jnp.einsum('tlcd,ldf->tlcf', row_block, expert_gate, preferred_element_ty...  6.26 us
  transfers between devices with their start and end apart: 1, of which 1 were waited for; matrix products, arithmetic and copies ran while one was open for 0% of the time, Pallas kernels for 0%

commit v1 on v0

--- a/solution.py
+++ b/solution.py
@@ -2,6 +2,20 @@
 import jax.numpy as jnp
 from jax import lax
 from jax.sharding import PartitionSpec as P
+
+
+def work_both_ways(x, axis, dim, make, out_dim):
+    ways, here, step = (lax.axis_size(axis), lax.axis_index(axis), x.shape[dim])
+    earlier, later = ([], [])
+    going_up = going_down = x
+    for far in range(ways // 2 + 1):
+        earlier.append(make(going_up, (here - far) % ways * step))
+        if 0 < far < ways - ways // 2:
+            later.append(make(going_down, (here + far) % ways * step))
+        going_up = lax.ppermute(going_up, axis, [(d, (d + 1) % ways) for d in range(ways)])
+        going_down = lax.ppermute(going_down, axis, [(d, (d - 1) % ways) for d in range(ways)])
+    line = jnp.concatenate([*earlier[::-1], *later], axis=out_dim)
+    return jnp.roll(line, (here - ways // 2) * earlier[0].shape[out_dim], axis=out_dim)
 
 
 def slot_tables(routing, route_gates, experts, capacity):
@@ -46,9 +60,14 @@
     experts = local_count * ep_count
     dispatch, combine = slot_tables(routing, route_gates, experts, capacity)
     dispatch_low = dispatch.astype(jnp.bfloat16)
-    whole = lax.all_gather(tokens, "tp", axis=1, tiled=True)
-    packed = jnp.einsum(
-        "tc,td->cd", dispatch_low, whole, preferred_element_type=jnp.float32
+    packed = work_both_ways(
+        tokens,
+        "tp",
+        1,
+        lambda part_2, at: jnp.einsum(
+            "tc,td->cd", dispatch_low, part_2, preferred_element_type=jnp.float32
+        ),
+        1,
     ).astype(jnp.bfloat16)
     everyone = lax.all_to_all(packed, "ep", split_axis=0, concat_axis=0, tiled=True)
     total_rows = everyone.shape[0]

time: 146 us -> 141 us (0.966)
  blocking collectives: 48.4 us -> 30.1 us
  waiting for transfers between devices: 53.2 us -> 58.7 us
  starting transfers between devices: 0.01 us -> 5.08 us
  matrix products: 24.6 us -> 26.1 us
    all_gather x1 -> x0, blocking collectives: 18.5 us -> none  [body(): whole = lax.all_gather(tokens, 'tp', axis=1, tiled=True)]
    ppermute x0 -> x3, waiting for transfers between devices: none -> 7.59 us  [the longest x2 7.58 us: work_both_ways(): lax.ppermute(going_up, axis, [(d, (d + 1) % ways) for d in range(ways)])]
    ppermute x0 -> x3, starting transfers between devices: none -> 5.08 us  [the longest x2 3.05 us: work_both_ways(): lax.ppermute(going_up, axis, [(d, (d + 1) % ways) for d in range(ways)])]
    reduce_scatter x1, waiting for transfers between devices: 53.2 us -> 51.1 us  [body(): lax.psum_scatter(part.reshape(columns // tp_count * lax.axis_size('tp'),...]
    dot_general x1 -> x4, matrix products: 0.52 us -> 2 us  [body(): jnp.einsum('tc,td->cd', dispatch_low, part_2, preferred_element_type=jnp....]
  transfers between devices with their start and end apart: 1 -> 4, of which waited for: 1 -> 3; matrix products, arithmetic and copies ran while one was open for 0% -> 4% of each run, Pallas kernels for 0% -> 0%
where the time goes in v1:
time: 141 us; the launch traced here: 140 us
  waiting for transfers between devices  58.7 us (42%)
  blocking collectives  30.1 us (21%)
  matrix products  26.1 us (19%)
  between operations  13.5 us (10%)
  starting transfers between devices  5.08 us (4%)
  other arithmetic  3.98 us (3%)
  local copies, waits for them, and re-layouts  2.84 us (2%)
    reduce_scatter x1, waiting for transfers between devices, body(): lax.psum_scatter(part.reshape(columns // tp_count * lax.axis_size('tp'),...  51.1 us
    all_to_all x1, blocking collectives, body(): lax.all_to_all(packed, 'ep', split_axis=0, concat_axis=0, tiled=True)  20.7 us
    all_to_all x1, blocking collectives, body(): lax.all_to_all(expert_out, 'ep', split_axis=0, concat_axis=0, tiled=True)  9.41 us
    dot_general x1, matrix products, body(): jnp.einsum('tlcf,lfd->dtlc', hidden, expert_down, preferred_element_type=...  9.01 us
    dot_general x1, matrix products, hidden_rows(): jnp.einsum('tlcd,ldf->tlcf', row_block, expert_up, preferred_element_type...  7.89 us
    ppermute x2, waiting for transfers between devices, work_both_ways(): lax.ppermute(going_up, axis, [(d, (d + 1) % ways) for d in range(ways)])  7.58 us
    dot_general x1, matrix products, hidden_rows(): jnp.einsum('tlcd,ldf->tlcf', row_block, expert_gate, preferred_element_ty...  6.25 us
    ppermute x2, starting transfers between devices, work_both_ways(): lax.ppermute(going_up, axis, [(d, (d + 1) % ways) for d in range(ways)])  3.05 us
  transfers between devices with their start and end apart: 4, of which 3 were waited for; matrix products, arithmetic and copies ran while one was open for 4% of the time, Pallas kernels for 0%

profile of v1, /device:TPU:0, one launch (start us, length us, event | category | flops | bytes accessed | tf_op | source)
XLA Modules:
  0.0 140.3 jit_solution(15480073419589309196)
XLA Ops:
  6.5 3.1 %collective-permute-start = (bf16[96,768]{1,0:T(8,128)(2,1)}, bf16[96,768]{1,0:T(8,128)(2,1)S(1)}, u32[]{:S(2)}, u32[]{:S(2)}) collective-permute-start(bf16[96,768]{1,0:T(8,128)(2,1)} %param.6), channel_id=1, source_target_pairs={{0,4},{4,8},{8,12},{12,0},{1,5},{5,9},{9,13},{13,1},{2,6},{6,10},{... | collective-permute-start | bytes 442376 | tf_op jit(solution)/shard_map/ppermute | solution.py:15
  9.6 2.0 %collective-permute-start.2 = (bf16[96,768]{1,0:T(8,128)(2,1)}, bf16[96,768]{1,0:T(8,128)(2,1)S(1)}, u32[]{:S(2)}, u32[]{:S(2)}) collective-permute-start(bf16[96,768]{1,0:T(8,128)(2,1)} %param.6), channel_id=1, source_target_pairs={{0,12},{4,0},{8,4},{12,8},{1,13},{5,1},{9,5},{13,9},{2,14},{6,2},{... | collective-permute-start | bytes 442376 | tf_op jit(solution)/shard_map/ppermute | solution.py:16
  11.6 0.8 copy.23
  12.4 0.1 eq.40
  12.6 1.2 reduce-window.6
  13.8 0.1 slice.12
  13.9 0.1 copy.24
  14.0 0.1 copy.25
  14.1 0.1 add_bitcast_fusion
  14.2 0.1 reduce_sum.30
  14.4 0.1 copy.26
  14.4 2.1 %collective-permute-done = bf16[96,768]{1,0:T(8,128)(2,1)S(1)} collective-permute-done((bf16[96,768]{1,0:T(8,128)(2,1)}, bf16[96,768]{1,0:T(8,128)(2,1)S(1)}, u32[]{:S(2)}, u32[]{:S(2)}) %collective-permute-start) | collective-permute-done | bytes 147488 | tf_op jit(solution)/shard_map/ppermute | solution.py:15
  16.6 0.7 multiply_add_fusion
  17.3 0.8 convert_reduce_fusion
  18.1 5.4 %collective-permute-done.1 = bf16[96,768]{1,0:T(8,128)(2,1)S(1)} collective-permute-done((bf16[96,768]{1,0:T(8,128)(2,1)S(1)}, bf16[96,768]{1,0:T(8,128)(2,1)S(1)}, u32[]{:S(2)}, u32[]{:S(2)}) %collective-permute-start.1) | collective-permute-done | bytes 147488 | tf_op jit(solution)/shard_map/ppermute | solution.py:15
  23.5 0.3 constant_dynamic-update-slice_fusion.7
  23.8 0.3 constant_dynamic-update-slice_fusion.6
  24.1 1.2 constant_dynamic-update-slice_fusion.5
  25.3 0.3 constant_dynamic-update-slice_fusion.4
  25.7 0.5 dynamic-slice_convert_fusion
  26.2 0.4 all_to_all.14
  26.6 20.7 %all_to_all.21 = bf16[4,54,3072]{2,1,0:T(8,128)(2,1)S(1)} all-to-all(bf16[4,54,3072]{2,1,0:T(8,128)(2,1)S(1)} %all_to_all.14), channel_id=1, replica_groups=mesh['rep'=2,'tp'=4,'ep'=4] {'ep'}, dimensions={0} | all-to-all | bytes 2654208 | tf_op jit(solution)/shard_map/all_to_all | solution.py:72
  47.3 6.3 %fusion.9 = f32[4,1,54,2048]{3,2,0,1:T(8,128)S(1)} fusion(bf16[4,54,3072]{2,1,0:T(8,128)(2,1)S(1)} %all_to_all.21, bf16[1,3072,2048]{2,1,0:T(8,128)(2,1)} %param.9), kind=kOutput, calls=%fused_computation.7 | convolution fusion | flops 2717908992 | bytes 15679488 | tf_op jit(solution)/shard_map/tlcd,ldf->tlcf/dot_general | solution.py:47
  53.6 7.9 %fusion.18 = bf16[4,1,54,2048]{3,2,0,1:T(8,128)(2,1)S(1)} fusion(bf16[4,54,3072]{2,1,0:T(8,128)(2,1)S(1)} %all_to_all.21, bf16[1,3072,2048]{2,1,0:T(8,128)(2,1)} %param.10, f32[4,1,54,2048]{3,2,0,1:T(8,128)S(1)} %fusion.9), kind=kOutput, calls=%fused_computation.11 | convolution fusion | flops 2720563200 | bytes 16564224 | tf_op jit(solution)/shard_map/tlcd,ldf->tlcf/dot_general | solution.py:50
  61.5 0.2 dot_general.46
  61.7 9.0 %fusion.6 = f32[3072,216]{0,1:T(8,128)} fusion(bf16[216,2048]{1,0:T(8,128)(2,1)S(1)} %dot_general.46, bf16[1,2048,3072]{2,1,0:T(8,128)(2,1)} %param.11), kind=kOutput, calls=%fused_computation.6 | convolution fusion | flops 2717908992 | bytes 16121856 | tf_op jit(solution)/shard_map/tlcf,lfd->dtlc/dot_general | solution.py:76
  70.7 51.1 %reduce-scatter.2.cloned.1.call-done = f32[768,216]{0,1:T(8,128)} async-done(((f32[3072,216]{0,1:T(8,128)}), f32[768,216]{0,1:T(8,128)}) %reduce-scatter.2.cloned.1.call-update) | async-done | bytes 663568 | tf_op jit(solution)/shard_map/reduce_scatter | solution.py:77
  121.8 1.1 convert_bitcast_fusion
  122.9 0.1 all_to_all.16
  123.0 9.4 %all_to_all.22 = bf16[4,54,768]{2,1,0:T(8,128)(2,1)S(1)} all-to-all(bf16[4,54,768]{2,1,0:T(8,128)(2,1)S(1)} %all_to_all.16), channel_id=1, replica_groups=mesh['rep'=2,'tp'=4,'ep'=4] {'ep'}, dimensions={0} | all-to-all | bytes 663552 | tf_op jit(solution)/shard_map/all_to_all | solution.py:85
  132.5 0.1 all_to_all.18
  132.5 1.0 convolution_convert_fusion
  (15 shorter events, 0.3 us)
Async XLA Ops:
  6.5 115.3 %reduce-scatter.2.cloned.1.call-start = ((), (), s32[]{:S(2)}) async-start(), calls=%async_computation.3 | async-start | bytes 3317760 | tf_op jit(solution)/shard_map/reduce_scatter | solution.py:77
  6.5 10.0 %collective-permute-start = (bf16[96,768]{1,0:T(8,128)(2,1)}, bf16[96,768]{1,0:T(8,128)(2,1)S(1)}, u32[]{:S(2)}, u32[]{:S(2)}) collective-permute-start(bf16[96,768]{1,0:T(8,128)(2,1)} %param.6), channel_id=1, source_target_pairs={{0,4},{4,8},{8,12},{12,0},{1,5},{5,9},{9,13},{13,1},{2,6},{6,10},{... | collective-permute-start | bytes 442376 | tf_op jit(solution)/shard_map/ppermute | solution.py:15
  9.6 15.7 %collective-permute-start.2 = (bf16[96,768]{1,0:T(8,128)(2,1)}, bf16[96,768]{1,0:T(8,128)(2,1)S(1)}, u32[]{:S(2)}, u32[]{:S(2)}) collective-permute-start(bf16[96,768]{1,0:T(8,128)(2,1)} %param.6), channel_id=1, source_target_pairs={{0,12},{4,0},{8,4},{12,8},{1,13},{5,1},{9,5},{13,9},{2,14},{6,2},{... | collective-permute-start | bytes 442376 | tf_op jit(solution)/shard_map/ppermute | solution.py:16
  16.6 6.9 %collective-permute-start.1 = (bf16[96,768]{1,0:T(8,128)(2,1)S(1)}, bf16[96,768]{1,0:T(8,128)(2,1)S(1)}, u32[]{:S(2)}, u32[]{:S(2)}) collective-permute-start(bf16[96,768]{1,0:T(8,128)(2,1)S(1)} %collective-permute-done), channel_id=1, source_target_pairs={{0,4},{4,8},{8,12},{12,0},{1,5},{5,9},{9,13},{13,1},{2,6},{6,10},{... | collective-permute-start | bytes 442376 | tf_op jit(solution)/shard_map/ppermute | solution.py:15
Sparse Core Ops, SparseCore 0:
  70.9 50.9 reduce-scatter.1
